TPU v7x, 8 devices: a whole 2x2x1 slice. The times are simulated.
8 devices in a mesh: dp: 1 (over z), tp: 8 (over y, x, core).
Axes of the slice: x: 2, y: 2, z: 1, core: 2. Of those that a mesh axis runs over, the one named last changes fastest.
Arguments:
- x: bfloat16 [32, 1024], P('dp')
- k_cache: bfloat16 [32, 8192, 16, 64], P('dp', None, 'tp')
- v_cache: bfloat16 [32, 8192, 16, 64], P('dp', None, 'tp')
- seq_lens: int32 [32], P('dp')
- nbr_enc: bfloat16 [32, 256, 1024], P('dp', 'tp')
- ln1_gain: float32 [1024], replicated
- ln1_bias: float32 [1024], replicated
- w_q: bfloat16 [1024, 1024], P(None, 'tp')
- w_k: bfloat16 [1024, 1024], P(None, 'tp')
- w_v: bfloat16 [1024, 1024], P(None, 'tp')
- w_o: bfloat16 [1024, 1024], P('tp')
- ln2_gain: float32 [1024], replicated
- ln2_bias: float32 [1024], replicated
- wq_c: bfloat16 [1024, 1024], P(None, 'tp')
- wk_c: bfloat16 [1024, 1024], P(None, 'tp')
- wv_c: bfloat16 [1024, 1024], P(None, 'tp')
- wo_c: bfloat16 [1024, 1024], P('tp')
- ln3_gain: float32 [1024], replicated
- ln3_bias: float32 [1024], replicated
- w_up: bfloat16 [1024, 4096], P(None, 'tp')
- w_down: bfloat16 [4096, 1024], P('tp')
Outputs:
- output 1: bfloat16 [32, 1024], P('dp')
- output 2: bfloat16 [32, 16, 64], P('dp', 'tp')
- output 3: bfloat16 [32, 16, 64], P('dp', 'tp')
All inputs are finite; a program needn't handle non-finite values.
Results may differ from a plain program's by a relative error of at most 0.0159068.
Values are sent between devices in bfloat16 or wider.
A program may use at most 1 GiB of HBM per device.

v0:
```python
import jax
import jax.numpy as jnp
from jax import lax
from jax.sharding import PartitionSpec as P

LN_EPS = 1e-5


def layer_norm(values, ln_gain, ln_bias):
    row_mean = jnp.mean(values, axis=-1, keepdims=True)
    centred = values - row_mean
    row_var = jnp.mean(jnp.square(centred), axis=-1, keepdims=True)
    return (centred * lax.rsqrt(row_var + LN_EPS) * ln_gain + ln_bias).astype(jnp.bfloat16)


def project(operand, weight):
    return jnp.dot(operand, weight, preferred_element_type=jnp.float32).astype(jnp.bfloat16)


def self_attention(q_new, k_new, v_new, k_cache, v_cache, seq_lens, q_scale):
    ctx_len = k_cache.shape[1]
    s_old = jnp.einsum('bhd,bthd->bht', q_new, k_cache, preferred_element_type=jnp.float32) * q_scale
    valid = jnp.arange(ctx_len)[None, None, :] < seq_lens[:, None, None]
    s_old = jnp.where(valid, s_old, -1e30)
    s_new = jnp.einsum('bhd,bhd->bh', q_new, k_new, preferred_element_type=jnp.float32) * q_scale
    row_max = jnp.maximum(jnp.max(s_old, axis=-1), s_new)
    e_old = jnp.exp(s_old - row_max[..., None])
    e_new = jnp.exp(s_new - row_max)
    row_sum = jnp.sum(e_old, axis=-1) + e_new
    p_old = (e_old / row_sum[..., None]).astype(jnp.bfloat16)
    p_new = (e_new / row_sum).astype(jnp.bfloat16)
    head_out = jnp.einsum('bht,bthd->bhd', p_old, v_cache, preferred_element_type=jnp.float32) + p_new.astype(jnp.float32)[..., None] * v_new.astype(jnp.float32)
    return head_out.astype(jnp.bfloat16)


def cross_attention(q_cross, k_nbr, v_nbr, q_scale):
    scores = jnp.einsum('bhd,bnhd->bhn', q_cross, k_nbr, preferred_element_type=jnp.float32) * q_scale
    probs = jax.nn.softmax(scores, axis=-1).astype(jnp.bfloat16)
    return jnp.einsum('bhn,bnhd->bhd', probs, v_nbr, preferred_element_type=jnp.float32).astype(jnp.bfloat16)


def local_step(x, k_cache, v_cache, seq_lens, nbr_enc, ln1_gain, ln1_bias, w_q, w_k, w_v, w_o, ln2_gain, ln2_bias, wq_c, wk_c, wv_c, wo_c, ln3_gain, ln3_bias, w_up, w_down):
    batch = x.shape[0]
    heads = k_cache.shape[2]
    head_dim = k_cache.shape[3]
    q_scale = head_dim ** -0.5
    residual = x.astype(jnp.float32)
    a_norm = layer_norm(residual, ln1_gain, ln1_bias)
    q_new = project(a_norm, w_q).reshape(batch, heads, head_dim)
    k_new = project(a_norm, w_k).reshape(batch, heads, head_dim)
    v_new = project(a_norm, w_v).reshape(batch, heads, head_dim)
    self_out = self_attention(q_new, k_new, v_new, k_cache, v_cache, seq_lens, q_scale)
    self_part = project(self_out.reshape(batch, heads * head_dim), w_o)
    residual = residual + lax.psum(self_part, 'tp').astype(jnp.float32)
    c_norm = layer_norm(residual, ln2_gain, ln2_bias)
    q_cross = project(c_norm, wq_c).reshape(batch, heads, head_dim)
    enc_all = lax.all_gather(nbr_enc, 'tp', axis=1, tiled=True)
    nbr_tokens = enc_all.shape[1]
    k_nbr = jnp.einsum('bne,ef->bnf', enc_all, wk_c, preferred_element_type=jnp.float32).astype(jnp.bfloat16).reshape(batch, nbr_tokens, heads, head_dim)
    v_nbr = jnp.einsum('bne,ef->bnf', enc_all, wv_c, preferred_element_type=jnp.float32).astype(jnp.bfloat16).reshape(batch, nbr_tokens, heads, head_dim)
    cross_out = cross_attention(q_cross, k_nbr, v_nbr, q_scale)
    cross_part = project(cross_out.reshape(batch, heads * head_dim), wo_c)
    residual = residual + lax.psum(cross_part, 'tp').astype(jnp.float32)
    m_norm = layer_norm(residual, ln3_gain, ln3_bias)
    hidden = jax.nn.gelu(jnp.dot(m_norm, w_up, preferred_element_type=jnp.float32), approximate=False).astype(jnp.bfloat16)
    mlp_part = project(hidden, w_down)
    layer_out = (residual + lax.psum(mlp_part, 'tp').astype(jnp.float32)).astype(jnp.bfloat16)
    return layer_out, k_new, v_new


def solution(mesh):
    row_spec = P('dp', None)
    cache_spec = P('dp', None, 'tp', None)
    head_spec = P('dp', 'tp', None)
    vec_spec = P(None)
    col_split = P(None, 'tp')
    row_split = P('tp', None)
    in_specs = (row_spec, cache_spec, cache_spec, P('dp'), P('dp', 'tp', None), vec_spec, vec_spec, col_split, col_split, col_split, row_split, vec_spec, vec_spec, col_split, col_split, col_split, row_split, vec_spec, vec_spec, col_split, row_split)
    out_specs = (row_spec, head_spec, head_spec)
    return jax.shard_map(local_step, mesh=mesh, in_specs=in_specs, out_specs=out_specs, check_vma=False)
```

profile of v0, /device:TPU:0, one launch (start us, length us, event | category | flops | bytes accessed | tf_op | source)
XLA Modules:
  0.0 325.1 jit_solution(5146212198730585724)
XLA Ops:
  7.2 0.0 all-reduce.4.cloned.1.call-start
  7.2 1.0 convert_reduce_fusion
  8.3 1.0 fusion.17
  9.3 1.3 convolution_convert_fusion.8
  10.6 0.1 reshape.98
  10.7 0.1 reshape.119
  10.7 1.2 convolution_convert_fusion.7
  12.0 0.1 reshape.99
  12.1 0.1 fusion.44
  12.2 0.1 copy.34
  12.3 0.9 iota_compare_fusion
  13.1 23.4 %fusion.116 = f32[32,2,1,8192]{3,2,1,0:T(1,128)S(1)} fusion(bf16[32,2,64,1]{2,3,1,0:T(2,128)(2,1)S(1)} %reshape.119, bf16[32,8192,2,64]{1,3,2,0:T(8,128)(2,1)} %param.22), kind=kOutput, calls=%fused_computation.155 | convolution fusion | flops 67108864 | bytes 69214208 | tf_op jit(solution)/shard_map/bhd,bthd->bht/dot_general | solution.py:22
  36.6 1.4 fusion.6
  38.0 1.6 fusion.5
  39.7 2.7 fusion.12
  42.4 0.1 copy.26
  42.5 1.2 convolution_convert_fusion.6
  43.6 0.1 reshape.100
  43.8 26.4 %fusion.3 = f32[32,2,1,64]{3,2,1,0:T(1,128)S(1)} fusion(bf16[32,8192,2,64]{1,3,2,0:T(8,128)(2,1)} %param.23, bf16[32,2,8192,1]{2,0,1,3:T(8,128)(2,1)} %fusion.12), kind=kOutput, calls=%fused_computation.4 | convolution fusion | flops 67108864 | bytes 68173824 | tf_op jit(solution)/shard_map/bht,bthd->bhd/dot_general | solution.py:32
  70.2 0.1 add_convert_fusion.9
  70.3 0.1 reshape.101
  70.4 0.8 convolution_convert_fusion.4
  71.2 0.0 all-reduce.4.cloned.1.call-update
  71.3 0.0 all-gather.2.cloned.1.call-start
  71.3 0.7 all-gather.2.cloned.1.call-update
  72.0 0.2 all-reduce.6.cloned.1.call-start
  72.2 43.9 %all-reduce.4.cloned.1.call-done = bf16[32,1024]{1,0:T(8,128)(2,1)} async-done(((bf16[32,1024]{1,0:T(8,128)(2,1)}), bf16[32,1024]{1,0:T(8,128)(2,1)}) %all-reduce.4.cloned.1.call-update) | async-done | bytes 65552 | tf_op jit(solution)/shard_map/psum | solution.py:54
  116.2 1.0 fusion.21
  117.1 1.0 multiply_reduce_fusion.1
  118.2 1.1 convolution_convert_fusion.5
  119.3 0.7 reshape.121
  120.0 81.6 %all-gather.2.cloned.1.call-done = bf16[32,256,1024]{2,1,0:T(8,128)(2,1)} async-done(((bf16[32,32,1024]{2,1,0:T(8,128)(2,1)}), bf16[32,256,1024]{2,1,0:T(8,128)(2,1)}) %all-gather.2.cloned.1.call-update) | async-done | bytes 16777232 | tf_op jit(solution)/shard_map/all_gather | solution.py:57
  201.6 11.3 %convolution_convert_fusion.1 = bf16[32,256,128]{1,2,0:T(8,128)(2,1)S(1)} fusion(bf16[32,256,1024]{2,1,0:T(8,128)(2,1)} %all-gather.2.cloned.1.call-done, bf16[1024,128]{1,0:T(8,128)(2,1)S(1)} %copy-done.4), kind=kOutput, calls=%fused_computation.9 | convolution fusion | flops 2148532224 | bytes 19136512 | tf_op jit(solution)/shard_map/bne,ef->bnf/dot_general | solution.py:59
  212.9 1.2 fusion.117
  214.1 0.8 fusion.11
  214.9 11.3 %convolution_convert_fusion = bf16[32,256,128]{1,2,0:T(8,128)(2,1)S(1)} fusion(bf16[32,256,1024]{2,1,0:T(8,128)(2,1)} %all-gather.2.cloned.1.call-done, bf16[1024,128]{1,0:T(8,128)(2,1)S(1)} %copy-done.5), kind=kOutput, calls=%fused_computation.8 | convolution fusion | flops 2148532224 | bytes 19136512 | tf_op jit(solution)/shard_map/bne,ef->bnf/dot_general | solution.py:60
  226.3 1.4 fusion.26
  227.7 0.1 reshape.105
  227.8 0.8 convolution_convert_fusion.3
  228.6 0.0 all-reduce.6.cloned.1.call-update
  228.7 0.0 all-reduce.8.cloned.1.call-start
  228.7 42.1 %all-reduce.6.cloned.1.call-done = bf16[32,1024]{1,0:T(8,128)(2,1)} async-done(((bf16[32,1024]{1,0:T(8,128)(2,1)}), bf16[32,1024]{1,0:T(8,128)(2,1)}) %all-reduce.6.cloned.1.call-update) | async-done | bytes 65552 | tf_op jit(solution)/shard_map/psum | solution.py:63
  270.8 1.0 fusion.112
  271.8 1.0 multiply_reduce_fusion
  272.9 2.6 convolution_convert_fusion.2
  275.5 0.0 all-reduce.8.cloned.1.call-update
  275.6 41.5 %all-reduce.8.cloned.1.call-done = bf16[32,1024]{1,0:T(8,128)(2,1)} async-done(((bf16[32,1024]{1,0:T(8,128)(2,1)}), bf16[32,1024]{1,0:T(8,128)(2,1)}) %all-reduce.8.cloned.1.call-update) | async-done | bytes 65552 | tf_op jit(solution)/shard_map/psum | solution.py:67
  317.1 1.5 add_convert_fusion
  (43 shorter events, 0.2 us)
Async XLA Ops:
  7.2 265.7 %copy-start = (bf16[512,1024]{1,0:T(8,128)(2,1)S(1)}, bf16[512,1024]{1,0:T(8,128)(2,1)}, u32[]{:S(2)}) copy-start(bf16[512,1024]{1,0:T(8,128)(2,1)} %param.41) | copy-start | bytes 3145732
  7.2 109.0 %all-reduce.4.cloned.1.call-start = ((), (), s32[]{:S(2)}) async-start(), calls=%async_computation | async-start | bytes 131072 | tf_op jit(solution)/shard_map/psum | solution.py:54
  12.1 24.5 %copy-start.8 = (bf16[32,2,64]{2,1,0:T(2,128)(2,1)}, bf16[32,2,64]{2,1,0:T(2,128)(2,1)S(1)}, u32[]{:S(2)}) copy-start(bf16[32,2,64]{2,1,0:T(2,128)(2,1)S(1)} %reshape.99) | copy-start | bytes 24580
  39.7 2.8 copy-start.1
  39.7 2.8 copy-start.11
  39.7 2.8 copy-start.12
  43.7 26.5 %copy-start.9 = (bf16[32,2,64]{2,1,0:T(2,128)(2,1)}, bf16[32,2,64]{2,1,0:T(2,128)(2,1)S(1)}, u32[]{:S(2)}) copy-start(bf16[32,2,64]{2,1,0:T(2,128)(2,1)S(1)} %reshape.100) | copy-start | bytes 24580
  43.7 26.7 %copy-start.6 = (bf16[128,1024]{1,0:T(8,128)(2,1)S(1)}, bf16[128,1024]{1,0:T(8,128)(2,1)}, u32[]{:S(2)}) copy-start(bf16[128,1024]{1,0:T(8,128)(2,1)} %param.31) | copy-start | bytes 786436
  70.2 48.0 %copy-start.10 = (bf16[1024,128]{1,0:T(8,128)(2,1)S(1)}, bf16[1024,128]{1,0:T(8,128)(2,1)}, u32[]{:S(2)}) copy-start(bf16[1024,128]{1,0:T(8,128)(2,1)} %param.34) | copy-start | bytes 786436
  70.2 48.0 %copy-start.13 = (f32[1024]{0:T(1024)S(1)}, f32[1024]{0:T(1024)}, u32[]{:S(2)}) copy-start(f32[1024]{0:T(1024)} %param.33) | copy-start | bytes 12292
  70.2 48.0 %copy-start.14 = (f32[1024]{0:T(1024)S(1)}, f32[1024]{0:T(1024)}, u32[]{:S(2)}) copy-start(f32[1024]{0:T(1024)} %param.32) | copy-start | bytes 12292
  70.2 131.4 %copy-start.4 = (bf16[1024,128]{1,0:T(8,128)(2,1)S(1)}, bf16[1024,128]{1,0:T(8,128)(2,1)}, u32[]{:S(2)}) copy-start(bf16[1024,128]{1,0:T(8,128)(2,1)} %param.35) | copy-start | bytes 786436
  71.3 130.3 %all-gather.2.cloned.1.call-start = ((), (), s32[]{:S(2)}) async-start(), calls=%async_computation.1 | async-start | bytes 18874368 | tf_op jit(solution)/shard_map/all_gather | solution.py:57
  72.0 198.8 %all-reduce.6.cloned.1.call-start = ((), (), s32[]{:S(2)}) async-start(), calls=%async_computation.2 | async-start | bytes 131072 | tf_op jit(solution)/shard_map/psum | solution.py:63
  212.9 2.0 copy-start.5
  226.2 1.6 copy-start.7
  226.2 44.5 %copy-start.2 = (bf16[32,1024]{1,0:T(8,128)(2,1)S(1)}, bf16[32,1024]{1,0:T(8,128)(2,1)}, u32[]{:S(2)}) copy-start(bf16[32,1024]{1,0:T(8,128)(2,1)} %all-reduce.4.cloned.1.call-done) | copy-start | bytes 196612
  226.2 46.6 %copy-start.15 = (f32[1024]{0:T(1024)S(1)}, f32[1024]{0:T(1024)}, u32[]{:S(2)}) copy-start(f32[1024]{0:T(1024)} %param.39) | copy-start | bytes 12292
  226.3 46.6 %copy-start.16 = (f32[1024]{0:T(1024)S(1)}, f32[1024]{0:T(1024)}, u32[]{:S(2)}) copy-start(f32[1024]{0:T(1024)} %param.38) | copy-start | bytes 12292
  228.7 88.4 %all-reduce.8.cloned.1.call-start = ((), (), s32[]{:S(2)}) async-start(), calls=%async_computation.3 | async-start | bytes 131072 | tf_op jit(solution)/shard_map/psum | solution.py:67
  270.8 46.3 %copy-start.3 = (bf16[32,1024]{1,0:T(8,128)(2,1)S(1)}, bf16[32,1024]{1,0:T(8,128)(2,1)}, u32[]{:S(2)}) copy-start(bf16[32,1024]{1,0:T(8,128)(2,1)} %all-reduce.6.cloned.1.call-done) | copy-start | bytes 196612
Sparse Core Ops, SparseCore 0:
  71.4 44.7 all-reduce.3
  118.0 83.5 all-gather.1
  228.8 41.9 all-reduce.5
  275.7 41.3 all-reduce.7
where the time goes:
time: 326 us; the launch traced here: 325 us
  waiting for transfers between devices  210 us (64%)
  matrix products  84.1 us (26%)
  other arithmetic  15.4 us (5%)
  between operations  14 us (4%)
    all_gather x1, waiting for transfers between devices, local_step(): enc_all = lax.all_gather(nbr_enc, 'tp', axis=1, tiled=True)  81.6 us
    psum x1, waiting for transfers between devices, local_step(): residual = residual + lax.psum(self_part, 'tp').astype(jnp.float32)  43.9 us
    psum x1, waiting for transfers between devices, local_step(): residual = residual + lax.psum(cross_part, 'tp').astype(jnp.float32)  42.1 us
    psum x1, waiting for transfers between devices, local_step(): lax.psum(mlp_part, 'tp').astype(jnp.float32)  41.5 us
    dot_general x1, matrix products, self_attention(): jnp.einsum('bht,bthd->bhd', p_old, v_cache, preferred_element_type=jnp.fl...  26.4 us
    dot_general x1, matrix products, self_attention(): jnp.einsum('bhd,bthd->bht', q_new, k_cache, preferred_element_type=jnp.fl...  23.4 us
    dot_general x1, matrix products, local_step(): jnp.einsum('bne,ef->bnf', enc_all, wv_c, preferred_element_type=jnp.float32)  11.3 us
    dot_general x1, matrix products, local_step(): jnp.einsum('bne,ef->bnf', enc_all, wk_c, preferred_element_type=jnp.float32)  11.3 us
  transfers between devices with their start and end apart: 4, of which 4 were waited for; matrix products, arithmetic and copies ran while one was open for 1% of the time, Pallas kernels for 0%

commit v1 on v0

--- a/solution.py
+++ b/solution.py
@@ -1,9 +1,17 @@
+import functools
+
 import jax
 import jax.numpy as jnp
 from jax import lax
+from jax.experimental import pallas as pl
+from jax.experimental.pallas import tpu as pltpu
 from jax.sharding import PartitionSpec as P
 
 LN_EPS = 1e-5
+CHUNK = 1024
+SLOTS = 8
+UNROLL = 2
+NEG = -1e30
 
 
 def layer_norm(values, ln_gain, ln_bias):
@@ -17,20 +25,206 @@
     return jnp.dot(operand, weight, preferred_element_type=jnp.float32).astype(jnp.bfloat16)
 
 
-def self_attention(q_new, k_new, v_new, k_cache, v_cache, seq_lens, q_scale):
-    ctx_len = k_cache.shape[1]
-    s_old = jnp.einsum('bhd,bthd->bht', q_new, k_cache, preferred_element_type=jnp.float32) * q_scale
-    valid = jnp.arange(ctx_len)[None, None, :] < seq_lens[:, None, None]
-    s_old = jnp.where(valid, s_old, -1e30)
-    s_new = jnp.einsum('bhd,bhd->bh', q_new, k_new, preferred_element_type=jnp.float32) * q_scale
-    row_max = jnp.maximum(jnp.max(s_old, axis=-1), s_new)
-    e_old = jnp.exp(s_old - row_max[..., None])
-    e_new = jnp.exp(s_new - row_max)
-    row_sum = jnp.sum(e_old, axis=-1) + e_new
-    p_old = (e_old / row_sum[..., None]).astype(jnp.bfloat16)
-    p_new = (e_new / row_sum).astype(jnp.bfloat16)
-    head_out = jnp.einsum('bht,bthd->bhd', p_old, v_cache, preferred_element_type=jnp.float32) + p_new.astype(jnp.float32)[..., None] * v_new.astype(jnp.float32)
-    return head_out.astype(jnp.bfloat16)
+def self_kernel(lens_ref, x_ref, gain_ref, bias_ref, wq_hbm, wk_hbm, wv_hbm, wo_hbm, k_hbm, v_hbm,
+                part_ref, know_ref, vnow_ref,
+                wq_buf, wk_buf, wv_buf, wo_buf, k_buf, v_buf, q_all, p_buf, acc, mx, sm, w_sem, k_sem, v_sem):
+    batch = x_ref.shape[0]
+    dim = k_buf.shape[1]
+    weights = [pltpu.make_async_copy(src, dst, w_sem.at[i]) for i, (src, dst) in enumerate(
+        ((wq_hbm, wq_buf), (wk_hbm, wk_buf), (wv_hbm, wv_buf), (wo_hbm, wo_buf)))]
+    for w in weights:
+        w.start()
+
+    def length(b):
+        return jnp.where(b < batch, lens_ref[jnp.minimum(b, batch - 1)], 64)
+
+    def advance(item):
+        b, j = item
+        more = (j + 1) * CHUNK < length(b)
+        return jnp.where(more, b, jnp.minimum(b + 1, batch)), jnp.where(more, j + 1, 0)
+
+    def view(item):
+        b, j = item
+        rem = jnp.minimum(length(b) - j * CHUNK, CHUNK)
+        size = pl.multiple_of((rem + 127) // 128 * 128, 128)
+        return jnp.minimum(b, batch - 1), pl.multiple_of(j * CHUNK, CHUNK), size
+
+    def fetch(hbm, buf, sem, item, slot):
+        b, start, size = view(item)
+        return pltpu.make_async_copy(hbm.at[b, :, pl.ds(start, size)], buf.at[slot, :, pl.ds(0, size)], sem.at[slot])
+
+    items = []
+    item = (jnp.int32(0), jnp.int32(0))
+    for _ in range(SLOTS):
+        items.append(item)
+        item = advance(item)
+    ahead = item
+    for s in range(SLOTS):
+        fetch(k_hbm, k_buf, k_sem, items[s], s).start()
+    v_buf[...] = jnp.zeros_like(v_buf)
+    for s in range(SLOTS):
+        fetch(v_hbm, v_buf, v_sem, items[s], s).start()
+
+    def count(b, total):
+        return total + (lens_ref[b] + CHUNK - 1) // CHUNK
+
+    groups = (lax.fori_loop(0, batch, count, jnp.int32(0)) + UNROLL - 1) // UNROLL
+
+    normed = layer_norm(x_ref[...].astype(jnp.float32), gain_ref[...], bias_ref[...])
+    for w in weights[:3]:
+        w.wait()
+    q_new = project(normed, wq_buf[...])
+    k_new = project(normed, wk_buf[...])
+    v_new = project(normed, wv_buf[...])
+    half = dim // 2
+    for h in range(2):
+        know_ref[:, h, :] = k_new[:, h * half:(h + 1) * half]
+        vnow_ref[:, h, :] = v_new[:, h * half:(h + 1) * half]
+    lane = lax.broadcasted_iota(jnp.int32, (batch, 8, dim), 2)
+    row = lax.broadcasted_iota(jnp.int32, (batch, 8, dim), 1)
+    own = (lane // half) == row
+    q_f = q_new.astype(jnp.float32)
+    q_wide = jnp.where(own, q_f[:, None, :], 0.0)
+    q_all[:batch] = q_wide.astype(jnp.bfloat16)
+    q_all[batch] = jnp.zeros((8, dim), jnp.bfloat16)
+    s_new = jnp.sum(q_wide * k_new.astype(jnp.float32)[:, None, :], axis=-1, keepdims=True) * (half ** -0.5)
+    mx[:batch] = jnp.broadcast_to(s_new, (batch, 8, dim))
+    sm[:batch] = jnp.ones((batch, 8, dim), jnp.float32)
+    acc[:batch] = jnp.broadcast_to(v_new.astype(jnp.float32)[:, None, :], (batch, 8, dim))
+    mx[batch] = jnp.zeros((8, dim), jnp.float32)
+    sm[batch] = jnp.ones((8, dim), jnp.float32)
+    acc[batch] = jnp.zeros((8, dim), jnp.float32)
+
+    spot = lax.broadcasted_iota(jnp.int32, (8, CHUNK), 1)
+    scale = half ** -0.5
+
+    def scores(item, slot):
+        b, j = item
+        s = jnp.dot(q_all[b], k_buf[slot], preferred_element_type=jnp.float32) * scale
+        s = jnp.where(spot < length(b) - j * CHUNK, s, NEG)
+        top = jnp.max(s, axis=-1, keepdims=True)
+        e = jnp.exp(s - top)
+        return e.astype(jnp.bfloat16), top, jnp.sum(e, axis=-1, keepdims=True)
+
+    def merge(item, p, top, total, slot):
+        b, _ = item
+        o = lax.dot_general(p, v_buf[slot], (((1,), (1,)), ((), ())), preferred_element_type=jnp.float32)
+        old = mx[b]
+        new = jnp.maximum(old, top)
+        keep = jnp.exp(old - new)
+        add = jnp.exp(top - new)
+        mx[b] = new
+        sm[b] = sm[b] * keep + total * add
+        acc[b] = acc[b] * keep + o * add
+
+    def stage_a(group_items, slot0):
+        out = []
+        for u in range(UNROLL):
+            out.append(scores(group_items[u], slot0 + u))
+        return out
+
+    def slot_of(group):
+        return lax.rem(group * UNROLL, SLOTS)
+
+    def flat(seq):
+        return tuple(x for pair in seq for x in pair)
+
+    def pair(vals):
+        return [(vals[2 * i], vals[2 * i + 1]) for i in range(UNROLL)]
+
+    cur = [items[u] for u in range(UNROLL)]
+    for u in range(UNROLL):
+        fetch(k_hbm, k_buf, k_sem, cur[u], u).wait()
+    first = stage_a(cur, 0)
+    for u in range(UNROLL):
+        p_buf[0, u] = first[u][0]
+    k_next = []
+    for u in range(UNROLL):
+        k_next.append(ahead)
+        ahead = advance(ahead)
+    for u in range(UNROLL):
+        fetch(k_hbm, k_buf, k_sem, k_next[u], u).start()
+    depth = SLOTS // UNROLL
+
+    def step(g, carry):
+        prev = pair(carry[:2 * UNROLL])
+        v_next = pair(carry[2 * UNROLL:4 * UNROLL])
+        walk = (carry[4 * UNROLL], carry[4 * UNROLL + 1])
+        stats = carry[4 * UNROLL + 2:]
+        now = []
+        it = advance(prev[-1])
+        for _ in range(UNROLL):
+            now.append(it)
+            it = advance(it)
+        slot_b = slot_of(g - 1)
+        slot_a = slot_of(g)
+        for u in range(UNROLL):
+            fetch(v_hbm, v_buf, v_sem, prev[u], slot_b + u).wait()
+            fetch(k_hbm, k_buf, k_sem, now[u], slot_a + u).wait()
+        before = lax.rem(g - 1, 2)
+        after = lax.rem(g, 2)
+        for u in range(UNROLL):
+            merge(prev[u], p_buf[before, u], stats[2 * u], stats[2 * u + 1], slot_b + u)
+        out = stage_a(now, slot_a)
+        for u in range(UNROLL):
+            p_buf[after, u] = out[u][0]
+        k_items = []
+        for _ in range(UNROLL):
+            k_items.append(walk)
+            walk = advance(walk)
+
+        @pl.when(g + depth <= groups)
+        def _():
+            for u in range(UNROLL):
+                fetch(k_hbm, k_buf, k_sem, k_items[u], slot_a + u).start()
+
+        @pl.when(g - 1 + depth < groups)
+        def _():
+            for u in range(UNROLL):
+                fetch(v_hbm, v_buf, v_sem, v_next[u], slot_b + u).start()
+
+        new_stats = tuple(x for u in range(UNROLL) for x in out[u][1:])
+        return flat(now) + flat(k_items) + walk + new_stats
+
+    init = flat(cur) + flat(k_next) + ahead + tuple(x for u in range(UNROLL) for x in first[u][1:])
+    lax.fori_loop(1, groups + 1, step, init)
+
+    lane2 = lax.broadcasted_iota(jnp.int32, (batch, dim), 1)
+    o0 = acc[:batch, 0, :] / sm[:batch, 0, :]
+    o1 = acc[:batch, 1, :] / sm[:batch, 1, :]
+    out = jnp.where(lane2 < half, o0, o1).astype(jnp.bfloat16)
+    weights[3].wait()
+    part_ref[...] = project(out, wo_buf[...])
+
+
+def self_attention(x, k_cache, v_cache, seq_lens, gain, bias, w_q, w_k, w_v, w_o):
+    batch, ctx, heads, head_dim = k_cache.shape
+    dim = heads * head_dim
+    model = x.shape[1]
+    k_t = k_cache.transpose(0, 2, 3, 1).reshape(batch, dim, ctx)
+    v_t = v_cache.transpose(0, 2, 3, 1).reshape(batch, dim, ctx)
+    vmem = pl.BlockSpec(memory_space=pltpu.VMEM)
+    anywhere = pl.BlockSpec(memory_space=pl.ANY)
+    f32, bf16 = jnp.float32, jnp.bfloat16
+    return pl.pallas_call(
+        self_kernel,
+        out_shape=(jax.ShapeDtypeStruct((batch, model), bf16),
+                   jax.ShapeDtypeStruct((batch, heads, head_dim), bf16),
+                   jax.ShapeDtypeStruct((batch, heads, head_dim), bf16)),
+        in_specs=[pl.BlockSpec(memory_space=pltpu.SMEM)] + [vmem] * 3 + [anywhere] * 6,
+        out_specs=(vmem, vmem, vmem),
+        scratch_shapes=[
+            pltpu.VMEM((model, dim), bf16), pltpu.VMEM((model, dim), bf16), pltpu.VMEM((model, dim), bf16),
+            pltpu.VMEM((dim, model), bf16),
+            pltpu.VMEM((SLOTS, dim, CHUNK), bf16), pltpu.VMEM((SLOTS, dim, CHUNK), bf16),
+            pltpu.VMEM((batch + 1, 8, dim), bf16),
+            pltpu.VMEM((2, UNROLL, 8, CHUNK), bf16),
+            pltpu.VMEM((batch + 1, 8, dim), f32), pltpu.VMEM((batch + 1, 8, dim), f32), pltpu.VMEM((batch + 1, 8, dim), f32),
+            pltpu.SemaphoreType.DMA((4,)), pltpu.SemaphoreType.DMA((SLOTS,)), pltpu.SemaphoreType.DMA((SLOTS,)),
+        ],
+        cost_estimate=pl.CostEstimate(flops=2 * 2 * batch * ctx * dim * 8, bytes_accessed=batch * ctx * dim * 2, transcendentals=0),
+        name="self_attention",
+    )(seq_lens, x, gain.reshape(1, model), bias.reshape(1, model), w_q, w_k, w_v, w_o, k_t, v_t)
 
 
 def cross_attention(q_cross, k_nbr, v_nbr, q_scale):
@@ -45,12 +239,7 @@
     head_dim = k_cache.shape[3]
     q_scale = head_dim ** -0.5
     residual = x.astype(jnp.float32)
-    a_norm = layer_norm(residual, ln1_gain, ln1_bias)
-    q_new = project(a_norm, w_q).reshape(batch, heads, head_dim)
-    k_new = project(a_norm, w_k).reshape(batch, heads, head_dim)
-    v_new = project(a_norm, w_v).reshape(batch, heads, head_dim)
-    self_out = self_attention(q_new, k_new, v_new, k_cache, v_cache, seq_lens, q_scale)
-    self_part = project(self_out.reshape(batch, heads * head_dim), w_o)
+    self_part, k_new, v_new = self_attention(x, k_cache, v_cache, seq_lens, ln1_gain, ln1_bias, w_q, w_k, w_v, w_o)
     residual = residual + lax.psum(self_part, 'tp').astype(jnp.float32)
     c_norm = layer_norm(residual, ln2_gain, ln2_bias)
     q_cross = project(c_norm, wq_c).reshape(batch, heads, head_dim)

time: 326 us -> 304 us (0.933)
  matrix products: 84.1 us -> 29 us
  Pallas kernels: 0 us -> 41.2 us
  other arithmetic: 15.4 us -> 6.4 us
    dot_general x2 -> x0, matrix products: 49.9 us -> none  [the longest x1 26.4 us: self_attention(): jnp.einsum('bht,bthd->bhd', p_old, v_cache, preferred_element_type=jnp.fl...]
    pallas_call x0 -> x1, Pallas kernels: none -> 41.2 us  [self_attention(): pl.pallas_call(self_kernel, out_shape=(jax.ShapeDtypeStruct((batch, model...]
    dot_general x7 -> x3, matrix products: 8.95 us -> 4.49 us  [project(): jnp.dot(operand, weight, preferred_element_type=jnp.float32)]
where the time goes in v1:
time: 304 us; the launch traced here: 301 us
  waiting for transfers between devices  211 us (69%)
  Pallas kernels  41.2 us (14%)
  matrix products  29 us (10%)
  between operations  13.9 us (5%)
  other arithmetic  6.4 us (2%)
    all_gather x1, waiting for transfers between devices, local_step(): enc_all = lax.all_gather(nbr_enc, 'tp', axis=1, tiled=True)  82.2 us
    psum x1, waiting for transfers between devices, local_step(): residual = residual + lax.psum(self_part, 'tp').astype(jnp.float32)  44.1 us
    psum x1, waiting for transfers between devices, local_step(): residual = residual + lax.psum(cross_part, 'tp').astype(jnp.float32)  42 us
    psum x1, waiting for transfers between devices, local_step(): lax.psum(mlp_part, 'tp').astype(jnp.float32)  41.5 us
    pallas_call x1, Pallas kernels, self_attention(): pl.pallas_call(self_kernel, out_shape=(jax.ShapeDtypeStruct((batch, model...  41.2 us
    dot_general x1, matrix products, local_step(): jnp.einsum('bne,ef->bnf', enc_all, wv_c, preferred_element_type=jnp.float32)  11.4 us
    dot_general x1, matrix products, local_step(): jnp.einsum('bne,ef->bnf', enc_all, wk_c, preferred_element_type=jnp.float32)  11.3 us
  transfers between devices with their start and end apart: 4, of which 4 were waited for; matrix products, arithmetic and copies ran while one was open for 1% of the time, Pallas kernels for 0%

profile of v1, /device:TPU:0, one launch (start us, length us, event | category | flops | bytes accessed | tf_op | source)
XLA Modules:
  0.0 301.4 jit_solution(8239434876965979699)
XLA Ops:
  7.2 0.0 copy-start
  7.2 0.0 all-reduce.4.cloned.1.call-start
  7.2 0.0 copy-start.1
  7.2 0.0 copy-start.5
  7.2 0.0 copy-start.6
  7.3 0.0 copy-start.7
  7.3 0.0 copy-start.3
  7.3 41.2 %self_attention.1 = (bf16[32,1024]{1,0:T(8,128)(2,1)}, bf16[32,2,64]{2,1,0:T(2,128)(2,1)}, bf16[32,2,64]{2,1,0:T(2,128)(2,1)}) custom-call(s32[32]{0:T(128)} %lens_ref.1, bf16[32,1024]{1,0:T(8,128)(2,1)} %x_ref.1, f32[1,1024]{1,0:T(1,128)} %bitcast.40, f32[1,1024]{1,0:T(1,128)} %bitcast.41, bf16[1024,128]{1,0:T(8,128)(2,1)} %wq_hbm.1, ...), custom_call_target="tpu_custom_call" | custom-call | flops 1073741824 | bytes 67108864 | tf_op jit(solution)/shard_map/self_attention/pallas_call | solution.py:209
  48.5 0.0 all-reduce.4.cloned.1.call-update
  48.5 0.0 all-gather.2.cloned.1.call-start
  48.6 0.7 all-gather.2.cloned.1.call-update
  49.3 0.0 all-reduce.6.cloned.1.call-start
  49.3 44.1 %all-reduce.4.cloned.1.call-done = bf16[32,1024]{1,0:T(8,128)(2,1)} async-done(((bf16[32,1024]{1,0:T(8,128)(2,1)}), bf16[32,1024]{1,0:T(8,128)(2,1)}) %all-reduce.4.cloned.1.call-update) | async-done | bytes 65552 | tf_op jit(solution)/shard_map/psum | solution.py:243
  93.4 0.0 copy-done.1
  93.4 1.0 fusion.9
  94.4 1.0 multiply_reduce_fusion.1
  95.5 0.0 copy-done.5
  95.5 0.0 copy-done.6
  95.5 0.0 copy-done.7
  95.5 1.1 convolution_convert_fusion.4
  96.6 0.1 reshape.75
  96.6 82.2 %all-gather.2.cloned.1.call-done = bf16[32,256,1024]{2,1,0:T(8,128)(2,1)} async-done(((bf16[32,32,1024]{2,1,0:T(8,128)(2,1)}), bf16[32,256,1024]{2,1,0:T(8,128)(2,1)}) %all-gather.2.cloned.1.call-update) | async-done | bytes 16777232 | tf_op jit(solution)/shard_map/all_gather | solution.py:246
  178.8 0.0 copy-done.3
  178.8 11.3 %convolution_convert_fusion.1 = bf16[32,256,128]{1,2,0:T(8,128)(2,1)S(1)} fusion(bf16[32,256,1024]{2,1,0:T(8,128)(2,1)} %all-gather.2.cloned.1.call-done, bf16[1024,128]{1,0:T(8,128)(2,1)S(1)} %copy-done.3), kind=kOutput, calls=%fused_computation.3 | convolution fusion | flops 2148532224 | bytes 19136512 | tf_op jit(solution)/shard_map/bne,ef->bnf/dot_general | solution.py:248
  190.2 0.4 fusion.97
  190.6 0.8 fusion.6
  191.4 0.0 copy-start.4
  191.4 0.0 copy-start.2
  191.4 0.0 copy-start.8
  191.4 0.0 copy-start.9
  191.4 11.4 %convolution_convert_fusion = bf16[32,256,128]{1,2,0:T(8,128)(2,1)S(1)} fusion(bf16[32,256,1024]{2,1,0:T(8,128)(2,1)} %all-gather.2.cloned.1.call-done, bf16[1024,128]{1,0:T(8,128)(2,1)} %param.36), kind=kOutput, calls=%fused_computation.2 | convolution fusion | flops 2148532224 | bytes 19136512 | tf_op jit(solution)/shard_map/bne,ef->bnf/dot_general | solution.py:249
  202.7 1.4 fusion.14
  204.2 0.1 reshape.67
  204.3 0.0 copy-done.4
  204.3 0.8 convolution_convert_fusion.3
  205.1 0.0 all-reduce.6.cloned.1.call-update
  205.1 0.0 all-reduce.8.cloned.1.call-start
  205.1 42.0 %all-reduce.6.cloned.1.call-done = bf16[32,1024]{1,0:T(8,128)(2,1)} async-done(((bf16[32,1024]{1,0:T(8,128)(2,1)}), bf16[32,1024]{1,0:T(8,128)(2,1)}) %all-reduce.6.cloned.1.call-update) | async-done | bytes 65552 | tf_op jit(solution)/shard_map/psum | solution.py:252
  247.2 0.0 copy-done.2
  247.2 1.0 fusion.96
  248.1 1.0 multiply_reduce_fusion
  249.2 0.0 copy-done
  249.2 0.0 copy-done.8
  249.2 0.0 copy-done.9
  249.2 2.6 convolution_convert_fusion.2
  251.8 0.0 all-reduce.8.cloned.1.call-update
  251.9 41.5 %all-reduce.8.cloned.1.call-done = bf16[32,1024]{1,0:T(8,128)(2,1)} async-done(((bf16[32,1024]{1,0:T(8,128)(2,1)}), bf16[32,1024]{1,0:T(8,128)(2,1)}) %all-reduce.8.cloned.1.call-update) | async-done | bytes 65552 | tf_op jit(solution)/shard_map/psum | solution.py:256
  293.4 1.5 add_convert_fusion
  (5 shorter events, 0.1 us)
Async XLA Ops:
  7.2 242.0 %copy-start = (bf16[512,1024]{1,0:T(8,128)(2,1)S(1)}, bf16[512,1024]{1,0:T(8,128)(2,1)}, u32[]{:S(2)}) copy-start(bf16[512,1024]{1,0:T(8,128)(2,1)} %param.41) | copy-start | bytes 3145732
  7.2 86.3 %all-reduce.4.cloned.1.call-start = ((), (), s32[]{:S(2)}) async-start(), calls=%async_computation | async-start | bytes 131072 | tf_op jit(solution)/shard_map/psum | solution.py:243
  7.2 86.2 %copy-start.1 = (bf16[32,1024]{1,0:T(8,128)(2,1)S(1)}, bf16[32,1024]{1,0:T(8,128)(2,1)}, u32[]{:S(2)}) copy-start(bf16[32,1024]{1,0:T(8,128)(2,1)} %x_ref.1) | copy-start | bytes 196612
  7.2 88.2 %copy-start.5 = (bf16[1024,128]{1,0:T(8,128)(2,1)S(1)}, bf16[1024,128]{1,0:T(8,128)(2,1)}, u32[]{:S(2)}) copy-start(bf16[1024,128]{1,0:T(8,128)(2,1)} %param.34) | copy-start | bytes 786436
  7.2 88.2 %copy-start.6 = (f32[1024]{0:T(1024)S(1)}, f32[1024]{0:T(1024)}, u32[]{:S(2)}) copy-start(f32[1024]{0:T(1024)} %param.33) | copy-start | bytes 12292
  7.3 88.2 %copy-start.7 = (f32[1024]{0:T(1024)S(1)}, f32[1024]{0:T(1024)}, u32[]{:S(2)}) copy-start(f32[1024]{0:T(1024)} %param.32) | copy-start | bytes 12292
  7.3 171.6 %copy-start.3 = (bf16[1024,128]{1,0:T(8,128)(2,1)S(1)}, bf16[1024,128]{1,0:T(8,128)(2,1)}, u32[]{:S(2)}) copy-start(bf16[1024,128]{1,0:T(8,128)(2,1)} %param.35) | copy-start | bytes 786436
  48.5 130.3 %all-gather.2.cloned.1.call-start = ((), (), s32[]{:S(2)}) async-start(), calls=%async_computation.1 | async-start | bytes 18874368 | tf_op jit(solution)/shard_map/all_gather | solution.py:246
  49.3 197.9 %all-reduce.6.cloned.1.call-start = ((), (), s32[]{:S(2)}) async-start(), calls=%async_computation.2 | async-start | bytes 131072 | tf_op jit(solution)/shard_map/psum | solution.py:252
  191.4 12.9 %copy-start.4 = (bf16[128,1024]{1,0:T(8,128)(2,1)S(1)}, bf16[128,1024]{1,0:T(8,128)(2,1)}, u32[]{:S(2)}) copy-start(bf16[128,1024]{1,0:T(8,128)(2,1)} %param.37) | copy-start | bytes 786436
  191.4 55.8 %copy-start.2 = (bf16[32,1024]{1,0:T(8,128)(2,1)S(1)}, bf16[32,1024]{1,0:T(8,128)(2,1)}, u32[]{:S(2)}) copy-start(bf16[32,1024]{1,0:T(8,128)(2,1)} %all-reduce.4.cloned.1.call-done) | copy-start | bytes 196612
  191.4 57.8 %copy-start.8 = (f32[1024]{0:T(1024)S(1)}, f32[1024]{0:T(1024)}, u32[]{:S(2)}) copy-start(f32[1024]{0:T(1024)} %param.39) | copy-start | bytes 12292
  191.4 57.8 %copy-start.9 = (f32[1024]{0:T(1024)S(1)}, f32[1024]{0:T(1024)}, u32[]{:S(2)}) copy-start(f32[1024]{0:T(1024)} %param.38) | copy-start | bytes 12292
  205.1 88.3 %all-reduce.8.cloned.1.call-start = ((), (), s32[]{:S(2)}) async-start(), calls=%async_computation.3 | async-start | bytes 131072 | tf_op jit(solution)/shard_map/psum | solution.py:256
Sparse Core Ops, SparseCore 0:
  48.6 44.7 all-reduce.3
  95.3 83.5 all-gather.1
  205.2 41.8 all-reduce.5
  252.0 41.3 all-reduce.7

commit v2 on v1

--- a/solution.py
+++ b/solution.py
@@ -9,7 +9,7 @@
 
 LN_EPS = 1e-5
 CHUNK = 1024
-SLOTS = 8
+SLOTS = 24
 UNROLL = 2
 NEG = -1e30
 
@@ -27,7 +27,8 @@
 
 def self_kernel(lens_ref, x_ref, gain_ref, bias_ref, wq_hbm, wk_hbm, wv_hbm, wo_hbm, k_hbm, v_hbm,
                 part_ref, know_ref, vnow_ref,
-                wq_buf, wk_buf, wv_buf, wo_buf, k_buf, v_buf, q_all, p_buf, acc, mx, sm, w_sem, k_sem, v_sem):
+                wq_buf, wk_buf, wv_buf, wo_buf, k_buf, v_buf, q_all, p_buf, acc, mx, sm, row_tab, start_tab, rem_tab,
+                w_sem, k_sem, v_sem):
     batch = x_ref.shape[0]
     dim = k_buf.shape[1]
     weights = [pltpu.make_async_copy(src, dst, w_sem.at[i]) for i, (src, dst) in enumerate(
@@ -35,40 +36,50 @@
     for w in weights:
         w.start()
 
-    def length(b):
-        return jnp.where(b < batch, lens_ref[jnp.minimum(b, batch - 1)], 64)
-
-    def advance(item):
-        b, j = item
-        more = (j + 1) * CHUNK < length(b)
-        return jnp.where(more, b, jnp.minimum(b + 1, batch)), jnp.where(more, j + 1, 0)
-
-    def view(item):
-        b, j = item
-        rem = jnp.minimum(length(b) - j * CHUNK, CHUNK)
-        size = pl.multiple_of((rem + 127) // 128 * 128, 128)
-        return jnp.minimum(b, batch - 1), pl.multiple_of(j * CHUNK, CHUNK), size
-
-    def fetch(hbm, buf, sem, item, slot):
-        b, start, size = view(item)
-        return pltpu.make_async_copy(hbm.at[b, :, pl.ds(start, size)], buf.at[slot, :, pl.ds(0, size)], sem.at[slot])
-
-    items = []
-    item = (jnp.int32(0), jnp.int32(0))
-    for _ in range(SLOTS):
-        items.append(item)
-        item = advance(item)
-    ahead = item
-    for s in range(SLOTS):
-        fetch(k_hbm, k_buf, k_sem, items[s], s).start()
+    def build(i, carry):
+        b, start, left = carry
+        row_tab[i] = b
+        start_tab[i] = start
+        rem_tab[i] = jnp.minimum(left, CHUNK)
+        more = left > CHUNK
+        nb = jnp.minimum(b + 1, batch)
+        fresh = jnp.where(nb < batch, lens_ref[jnp.minimum(nb, batch - 1)], 64)
+        return jnp.where(more, b, nb), jnp.where(more, start + CHUNK, 0), jnp.where(more, left - CHUNK, fresh)
+
+    def size_of(i):
+        return pl.multiple_of((rem_tab[i] + 127) // 128 * 128, 128)
+
+    def fetch(hbm, buf, sem, i, slot):
+        size = size_of(i)
+        b = jnp.minimum(row_tab[i], batch - 1)
+        return pltpu.make_async_copy(
+            hbm.at[b, :, pl.ds(pl.multiple_of(start_tab[i], CHUNK), size)], buf.at[slot, :, pl.ds(0, size)], sem.at[slot])
+
+    def fetch_k(i, slot):
+        return fetch(k_hbm, k_buf, k_sem, i, slot)
+
+    def fetch_v(i, slot):
+        return fetch(v_hbm, v_buf, v_sem, i, slot)
+
+    def open_k(i, carry):
+        carry = build(i, carry)
+        fetch_k(i, i).start(priority=0)
+        return carry
+
+    carry = lax.fori_loop(0, SLOTS, open_k, (jnp.int32(0), jnp.int32(0), lens_ref[0]))
     v_buf[...] = jnp.zeros_like(v_buf)
-    for s in range(SLOTS):
-        fetch(v_hbm, v_buf, v_sem, items[s], s).start()
+
+    def open_v(i, _):
+        fetch_v(i, i).start(priority=1)
+        return 0
+
+    lax.fori_loop(0, SLOTS, open_v, 0)
 
     def count(b, total):
         return total + (lens_ref[b] + CHUNK - 1) // CHUNK
 
     groups = (lax.fori_loop(0, batch, count, jnp.int32(0)) + UNROLL - 1) // UNROLL
+    lax.fori_loop(SLOTS, (groups + 1) * UNROLL, build, carry)
 
     normed = layer_norm(x_ref[...].astype(jnp.float32), gain_ref[...], bias_ref[...])
     for w in weights[:3]:
@@ -98,17 +109,18 @@
     spot = lax.broadcasted_iota(jnp.int32, (8, CHUNK), 1)
     scale = half ** -0.5
 
-    def scores(item, slot):
-        b, j = item
-        s = jnp.dot(q_all[b], k_buf[slot], preferred_element_type=jnp.float32) * scale
-        s = jnp.where(spot < length(b) - j * CHUNK, s, NEG)
+    def scores(i, slot):
+        s = jnp.dot(q_all[row_tab[i]], k_buf[slot], preferred_element_type=jnp.float32) * scale
+        s = jnp.where(spot < rem_tab[i], s, NEG)
         top = jnp.max(s, axis=-1, keepdims=True)
         e = jnp.exp(s - top)
         return e.astype(jnp.bfloat16), top, jnp.sum(e, axis=-1, keepdims=True)
 
-    def merge(item, p, top, total, slot):
-        b, _ = item
-        o = lax.dot_general(p, v_buf[slot], (((1,), (1,)), ((), ())), preferred_element_type=jnp.float32)
+    def weigh(p, slot):
+        return lax.dot_general(p, v_buf[slot], (((1,), (1,)), ((), ())), preferred_element_type=jnp.float32)
+
+    def merge(i, o, top, total):
+        b = row_tab[i]
         old = mx[b]
         new = jnp.maximum(old, top)
         keep = jnp.exp(old - new)
@@ -117,77 +129,47 @@
         sm[b] = sm[b] * keep + total * add
         acc[b] = acc[b] * keep + o * add
 
-    def stage_a(group_items, slot0):
-        out = []
-        for u in range(UNROLL):
-            out.append(scores(group_items[u], slot0 + u))
-        return out
-
-    def slot_of(group):
-        return lax.rem(group * UNROLL, SLOTS)
-
-    def flat(seq):
-        return tuple(x for pair in seq for x in pair)
-
-    def pair(vals):
-        return [(vals[2 * i], vals[2 * i + 1]) for i in range(UNROLL)]
-
-    cur = [items[u] for u in range(UNROLL)]
     for u in range(UNROLL):
-        fetch(k_hbm, k_buf, k_sem, cur[u], u).wait()
-    first = stage_a(cur, 0)
+        fetch_k(u, u).wait()
+    first = [scores(u, u) for u in range(UNROLL)]
     for u in range(UNROLL):
         p_buf[0, u] = first[u][0]
-    k_next = []
     for u in range(UNROLL):
-        k_next.append(ahead)
-        ahead = advance(ahead)
-    for u in range(UNROLL):
-        fetch(k_hbm, k_buf, k_sem, k_next[u], u).start()
+        fetch_k(SLOTS + u, u).start(priority=0)
     depth = SLOTS // UNROLL
 
-    def step(g, carry):
-        prev = pair(carry[:2 * UNROLL])
-        v_next = pair(carry[2 * UNROLL:4 * UNROLL])
-        walk = (carry[4 * UNROLL], carry[4 * UNROLL + 1])
-        stats = carry[4 * UNROLL + 2:]
-        now = []
-        it = advance(prev[-1])
-        for _ in range(UNROLL):
-            now.append(it)
-            it = advance(it)
-        slot_b = slot_of(g - 1)
-        slot_a = slot_of(g)
-        for u in range(UNROLL):
-            fetch(v_hbm, v_buf, v_sem, prev[u], slot_b + u).wait()
-            fetch(k_hbm, k_buf, k_sem, now[u], slot_a + u).wait()
+    def step(g, stats):
+        prev = (g - 1) * UNROLL
+        now = g * UNROLL
+        slot_b = lax.rem(prev, SLOTS)
+        slot_a = lax.rem(now, SLOTS)
+        for u in range(UNROLL):
+            fetch_k(now + u, slot_a + u).wait()
+        for u in range(UNROLL):
+            fetch_v(prev + u, slot_b + u).wait()
         before = lax.rem(g - 1, 2)
         after = lax.rem(g, 2)
-        for u in range(UNROLL):
-            merge(prev[u], p_buf[before, u], stats[2 * u], stats[2 * u + 1], slot_b + u)
-        out = stage_a(now, slot_a)
+        p_prev = [p_buf[before, u] for u in range(UNROLL)]
+        out = [scores(now + u, slot_a + u) for u in range(UNROLL)]
+        o_prev = [weigh(p_prev[u], slot_b + u) for u in range(UNROLL)]
+        for u in range(UNROLL):
+            merge(prev + u, o_prev[u], stats[2 * u], stats[2 * u + 1])
         for u in range(UNROLL):
             p_buf[after, u] = out[u][0]
-        k_items = []
-        for _ in range(UNROLL):
-            k_items.append(walk)
-            walk = advance(walk)
 
         @pl.when(g + depth <= groups)
         def _():
             for u in range(UNROLL):
-                fetch(k_hbm, k_buf, k_sem, k_items[u], slot_a + u).start()
+                fetch_k(now + SLOTS + u, slot_a + u).start(priority=0)
 
         @pl.when(g - 1 + depth < groups)
         def _():
             for u in range(UNROLL):
-                fetch(v_hbm, v_buf, v_sem, v_next[u], slot_b + u).start()
-
-        new_stats = tuple(x for u in range(UNROLL) for x in out[u][1:])
-        return flat(now) + flat(k_items) + walk + new_stats
-
-    init = flat(cur) + flat(k_next) + ahead + tuple(x for u in range(UNROLL) for x in first[u][1:])
-    lax.fori_loop(1, groups + 1, step, init)
+                fetch_v(prev + SLOTS + u, slot_b + u).start(priority=1)
+
+        return tuple(x for u in range(UNROLL) for x in out[u][1:])
+
+    lax.fori_loop(1, groups + 1, step, tuple(x for u in range(UNROLL) for x in first[u][1:]))
 
     lane2 = lax.broadcasted_iota(jnp.int32, (batch, dim), 1)
     o0 = acc[:batch, 0, :] / sm[:batch, 0, :]
@@ -201,6 +183,7 @@
     batch, ctx, heads, head_dim = k_cache.shape
     dim = heads * head_dim
     model = x.shape[1]
+    most = batch * (ctx // CHUNK) + 2 * UNROLL + SLOTS
     k_t = k_cache.transpose(0, 2, 3, 1).reshape(batch, dim, ctx)
     v_t = v_cache.transpose(0, 2, 3, 1).reshape(batch, dim, ctx)
     vmem = pl.BlockSpec(memory_space=pltpu.VMEM)
@@ -220,6 +203,7 @@
             pltpu.VMEM((batch + 1, 8, dim), bf16),
             pltpu.VMEM((2, UNROLL, 8, CHUNK), bf16),
             pltpu.VMEM((batch + 1, 8, dim), f32), pltpu.VMEM((batch + 1, 8, dim), f32), pltpu.VMEM((batch + 1, 8, dim), f32),
+            pltpu.SMEM((most,), jnp.int32), pltpu.SMEM((most,), jnp.int32), pltpu.SMEM((most,), jnp.int32),
             pltpu.SemaphoreType.DMA((4,)), pltpu.SemaphoreType.DMA((SLOTS,)), pltpu.SemaphoreType.DMA((SLOTS,)),
         ],
         cost_estimate=pl.CostEstimate(flops=2 * 2 * batch * ctx * dim * 8, bytes_accessed=batch * ctx * dim * 2, transcendentals=0),

time: 304 us -> 296 us (0.974)
  Pallas kernels: 41.2 us -> 34.4 us
    pallas_call x1, Pallas kernels: 41.2 us -> 34.4 us  [self_attention(): pl.pallas_call(self_kernel, out_shape=(jax.ShapeDtypeStruct((batch, model...]
where the time goes in v2:
time: 296 us; the launch traced here: 295 us
  waiting for transfers between devices  211 us (71%)
  Pallas kernels  34.4 us (12%)
  matrix products  29 us (10%)
  between operations  13.9 us (5%)
  other arithmetic  6.4 us (2%)
    all_gather x1, waiting for transfers between devices, local_step(): enc_all = lax.all_gather(nbr_enc, 'tp', axis=1, tiled=True)  82.2 us
    psum x1, waiting for transfers between devices, local_step(): residual = residual + lax.psum(self_part, 'tp').astype(jnp.float32)  44.1 us
    psum x1, waiting for transfers between devices, local_step(): residual = residual + lax.psum(cross_part, 'tp').astype(jnp.float32)  42.1 us
    psum x1, waiting for transfers between devices, local_step(): lax.psum(mlp_part, 'tp').astype(jnp.float32)  41.5 us
    pallas_call x1, Pallas kernels, self_attention(): pl.pallas_call(self_kernel, out_shape=(jax.ShapeDtypeStruct((batch, model...  34.4 us
    dot_general x1, matrix products, local_step(): jnp.einsum('bne,ef->bnf', enc_all, wv_c, preferred_element_type=jnp.float32)  11.4 us
    dot_general x1, matrix products, local_step(): jnp.einsum('bne,ef->bnf', enc_all, wk_c, preferred_element_type=jnp.float32)  11.3 us
  transfers between devices with their start and end apart: 4, of which 4 were waited for; matrix products, arithmetic and copies ran while one was open for 1% of the time, Pallas kernels for 0%

profile of v2, /device:TPU:0, one launch (start us, length us, event | category | flops | bytes accessed | tf_op | source)
XLA Modules:
  0.0 294.7 jit_solution(8486511000740543956)
XLA Ops:
  7.2 0.0 copy-start
  7.2 0.0 all-reduce.4.cloned.1.call-start
  7.2 0.0 copy-start.1
  7.2 0.0 copy-start.5
  7.2 0.0 copy-start.6
  7.3 0.0 copy-start.7
  7.3 0.0 copy-start.3
  7.3 34.4 %self_attention.1 = (bf16[32,1024]{1,0:T(8,128)(2,1)}, bf16[32,2,64]{2,1,0:T(2,128)(2,1)}, bf16[32,2,64]{2,1,0:T(2,128)(2,1)}) custom-call(s32[32]{0:T(128)} %lens_ref.1, bf16[32,1024]{1,0:T(8,128)(2,1)} %x_ref.1, f32[1,1024]{1,0:T(1,128)} %bitcast.40, f32[1,1024]{1,0:T(1,128)} %bitcast.41, bf16[1024,128]{1,0:T(8,128)(2,1)} %wq_hbm.1, ...), custom_call_target="tpu_custom_call" | custom-call | flops 1073741824 | bytes 67108864 | tf_op jit(solution)/shard_map/self_attention/pallas_call | solution.py:192
  41.7 0.0 all-reduce.4.cloned.1.call-update
  41.7 0.0 all-gather.2.cloned.1.call-start
  41.8 0.7 all-gather.2.cloned.1.call-update
  42.5 0.0 all-reduce.6.cloned.1.call-start
  42.5 44.1 %all-reduce.4.cloned.1.call-done = bf16[32,1024]{1,0:T(8,128)(2,1)} async-done(((bf16[32,1024]{1,0:T(8,128)(2,1)}), bf16[32,1024]{1,0:T(8,128)(2,1)}) %all-reduce.4.cloned.1.call-update) | async-done | bytes 65552 | tf_op jit(solution)/shard_map/psum | solution.py:227
  86.6 0.0 copy-done.1
  86.6 1.0 fusion.9
  87.6 1.0 multiply_reduce_fusion.1
  88.7 0.0 copy-done.5
  88.7 0.0 copy-done.6
  88.7 0.0 copy-done.7
  88.7 1.1 convolution_convert_fusion.4
  89.7 0.1 reshape.75
  89.8 82.2 %all-gather.2.cloned.1.call-done = bf16[32,256,1024]{2,1,0:T(8,128)(2,1)} async-done(((bf16[32,32,1024]{2,1,0:T(8,128)(2,1)}), bf16[32,256,1024]{2,1,0:T(8,128)(2,1)}) %all-gather.2.cloned.1.call-update) | async-done | bytes 16777232 | tf_op jit(solution)/shard_map/all_gather | solution.py:230
  172.0 0.0 copy-done.3
  172.0 11.3 %convolution_convert_fusion.1 = bf16[32,256,128]{1,2,0:T(8,128)(2,1)S(1)} fusion(bf16[32,256,1024]{2,1,0:T(8,128)(2,1)} %all-gather.2.cloned.1.call-done, bf16[1024,128]{1,0:T(8,128)(2,1)S(1)} %copy-done.3), kind=kOutput, calls=%fused_computation.3 | convolution fusion | flops 2148532224 | bytes 19136512 | tf_op jit(solution)/shard_map/bne,ef->bnf/dot_general | solution.py:232
  183.4 0.4 fusion.97
  183.7 0.8 fusion.6
  184.5 0.0 copy-start.4
  184.5 0.0 copy-start.2
  184.5 0.0 copy-start.8
  184.5 0.0 copy-start.9
  184.5 11.4 %convolution_convert_fusion = bf16[32,256,128]{1,2,0:T(8,128)(2,1)S(1)} fusion(bf16[32,256,1024]{2,1,0:T(8,128)(2,1)} %all-gather.2.cloned.1.call-done, bf16[1024,128]{1,0:T(8,128)(2,1)} %param.36), kind=kOutput, calls=%fused_computation.2 | convolution fusion | flops 2148532224 | bytes 19136512 | tf_op jit(solution)/shard_map/bne,ef->bnf/dot_general | solution.py:233
  195.9 1.4 fusion.14
  197.4 0.1 reshape.67
  197.4 0.0 copy-done.4
  197.5 0.8 convolution_convert_fusion.3
  198.2 0.0 all-reduce.6.cloned.1.call-update
  198.3 0.0 all-reduce.8.cloned.1.call-start
  198.3 42.1 %all-reduce.6.cloned.1.call-done = bf16[32,1024]{1,0:T(8,128)(2,1)} async-done(((bf16[32,1024]{1,0:T(8,128)(2,1)}), bf16[32,1024]{1,0:T(8,128)(2,1)}) %all-reduce.6.cloned.1.call-update) | async-done | bytes 65552 | tf_op jit(solution)/shard_map/psum | solution.py:236
  240.4 0.0 copy-done.2
  240.4 1.0 fusion.96
  241.4 1.0 multiply_reduce_fusion
  242.4 0.0 copy-done
  242.4 0.0 copy-done.8
  242.4 0.0 copy-done.9
  242.5 2.6 convolution_convert_fusion.2
  245.1 0.0 all-reduce.8.cloned.1.call-update
  245.1 41.5 %all-reduce.8.cloned.1.call-done = bf16[32,1024]{1,0:T(8,128)(2,1)} async-done(((bf16[32,1024]{1,0:T(8,128)(2,1)}), bf16[32,1024]{1,0:T(8,128)(2,1)}) %all-reduce.8.cloned.1.call-update) | async-done | bytes 65552 | tf_op jit(solution)/shard_map/psum | solution.py:240
  286.6 1.5 add_convert_fusion
  (5 shorter events, 0.1 us)
Async XLA Ops:
  7.2 235.3 %copy-start = (bf16[512,1024]{1,0:T(8,128)(2,1)S(1)}, bf16[512,1024]{1,0:T(8,128)(2,1)}, u32[]{:S(2)}) copy-start(bf16[512,1024]{1,0:T(8,128)(2,1)} %param.41) | copy-start | bytes 3145732
  7.2 79.4 %all-reduce.4.cloned.1.call-start = ((), (), s32[]{:S(2)}) async-start(), calls=%async_computation | async-start | bytes 131072 | tf_op jit(solution)/shard_map/psum | solution.py:227
  7.2 79.4 %copy-start.1 = (bf16[32,1024]{1,0:T(8,128)(2,1)S(1)}, bf16[32,1024]{1,0:T(8,128)(2,1)}, u32[]{:S(2)}) copy-start(bf16[32,1024]{1,0:T(8,128)(2,1)} %x_ref.1) | copy-start | bytes 196612
  7.2 81.4 %copy-start.5 = (bf16[1024,128]{1,0:T(8,128)(2,1)S(1)}, bf16[1024,128]{1,0:T(8,128)(2,1)}, u32[]{:S(2)}) copy-start(bf16[1024,128]{1,0:T(8,128)(2,1)} %param.34) | copy-start | bytes 786436
  7.2 81.4 %copy-start.6 = (f32[1024]{0:T(1024)S(1)}, f32[1024]{0:T(1024)}, u32[]{:S(2)}) copy-start(f32[1024]{0:T(1024)} %param.33) | copy-start | bytes 12292
  7.3 81.4 %copy-start.7 = (f32[1024]{0:T(1024)S(1)}, f32[1024]{0:T(1024)}, u32[]{:S(2)}) copy-start(f32[1024]{0:T(1024)} %param.32) | copy-start | bytes 12292
  7.3 164.8 %copy-start.3 = (bf16[1024,128]{1,0:T(8,128)(2,1)S(1)}, bf16[1024,128]{1,0:T(8,128)(2,1)}, u32[]{:S(2)}) copy-start(bf16[1024,128]{1,0:T(8,128)(2,1)} %param.35) | copy-start | bytes 786436
  41.7 130.3 %all-gather.2.cloned.1.call-start = ((), (), s32[]{:S(2)}) async-start(), calls=%async_computation.1 | async-start | bytes 18874368 | tf_op jit(solution)/shard_map/all_gather | solution.py:230
  42.5 197.9 %all-reduce.6.cloned.1.call-start = ((), (), s32[]{:S(2)}) async-start(), calls=%async_computation.2 | async-start | bytes 131072 | tf_op jit(solution)/shard_map/psum | solution.py:236
  184.5 12.9 %copy-start.4 = (bf16[128,1024]{1,0:T(8,128)(2,1)S(1)}, bf16[128,1024]{1,0:T(8,128)(2,1)}, u32[]{:S(2)}) copy-start(bf16[128,1024]{1,0:T(8,128)(2,1)} %param.37) | copy-start | bytes 786436
  184.5 55.9 %copy-start.2 = (bf16[32,1024]{1,0:T(8,128)(2,1)S(1)}, bf16[32,1024]{1,0:T(8,128)(2,1)}, u32[]{:S(2)}) copy-start(bf16[32,1024]{1,0:T(8,128)(2,1)} %all-reduce.4.cloned.1.call-done) | copy-start | bytes 196612
  184.5 57.9 %copy-start.8 = (f32[1024]{0:T(1024)S(1)}, f32[1024]{0:T(1024)}, u32[]{:S(2)}) copy-start(f32[1024]{0:T(1024)} %param.39) | copy-start | bytes 12292
  184.5 57.9 %copy-start.9 = (f32[1024]{0:T(1024)S(1)}, f32[1024]{0:T(1024)}, u32[]{:S(2)}) copy-start(f32[1024]{0:T(1024)} %param.38) | copy-start | bytes 12292
  198.3 88.3 %all-reduce.8.cloned.1.call-start = ((), (), s32[]{:S(2)}) async-start(), calls=%async_computation.3 | async-start | bytes 131072 | tf_op jit(solution)/shard_map/psum | solution.py:240
Sparse Core Ops, SparseCore 0:
  41.8 44.7 all-reduce.3
  88.5 83.5 all-gather.1
  198.4 41.9 all-reduce.5
  245.2 41.3 all-reduce.7
